TPU v7x, 32 devices: a whole 2x2x4 slice. The times are simulated.
32 devices in a mesh: wide: 16 (over z, x, core), lev: 2 (over y).
Axes of the slice: x: 2, y: 2, z: 4, core: 2. Of those that a mesh axis runs over, the one named last changes fastest.
Arguments:
- member_control: float32 [16, 16, 128], P('wide'), may hold values from -6 to 6
- static_control: float32 [8, 128, 1024], P('lev', 'wide'), may hold values from -6 to 6
- perturbations: bfloat16 [16, 8, 128, 1024], P(None, 'lev', 'wide'), may hold values from -6 to 6
- innovation: float32 [8, 128, 1024], P('lev', 'wide'), may hold values from -9 to 9
- diffusivity: float32 [8, 128, 1024], P('lev', 'wide'), may hold values from 0.05 to 0.15
- rows_factor: float32 [16, 16], replicated, may hold values from -1.5 to 1.5
- column_factor: float32 [128, 128], replicated, may hold values from -0.5 to 0.5
- ocean_mask: int32 [128, 1024], P('wide'), may hold values 0 or 1
- huber_blocks: int32 [8, 16, 128], P('lev', 'wide'), may hold values 0 or 1
- fold_map: int32 [1024], replicated, may hold values from 0 to 1023, as said below
Outputs:
- increment: float32 [8, 128, 1024], P('lev', 'wide')
- member_gradient: float32 [16, 16, 128], P('wide')
- static_gradient: float32 [8, 128, 1024], P('lev', 'wide')
Inputs may be any that keep to these rules, and one draw needn't show every extreme that they name: fold_map[fold_map[j]] = j and fold_map[j] != j for every column j.
All inputs are finite; a program needn't handle non-finite values. No bound on the sum of `ocean_mask` or of `huber_blocks` on one device may be relied on, other than what follows from the above.
Results may differ from a plain program's by a relative error of at most 0.0003.
Values sent between devices are 32-bit elements; how exact they have to be, the bound alone decides.
No kernel may reach another device: no remote copies, remote signals or barrier semaphores. Data moves between devices by JAX's collectives and lax.ppermute only.
A program may use at most 64 MiB of HBM per device.

v0:
```python
import jax
import jax.numpy as jnp
from jax import lax
from jax.sharding import PartitionSpec as P

REFINE = 8
STEPS = 3
HUBER_EDGE = 1.0
VERTICAL_WEIGHT = 0.5
PRECISE = lax.Precision.HIGHEST


def with_halo(array, sides, width):
    for axis, dim in sides:
        count, length = (lax.axis_size(axis), array.shape[dim])
        up = [(i, (i + 1) % count) for i in range(count - 1)]
        down = [(j, i) for i, j in up]
        last = lax.slice_in_dim(array, length - width, length, axis=dim)
        first = lax.slice_in_dim(array, 0, width, axis=dim)
        before = lax.ppermute(last, axis, up)
        after = lax.ppermute(first, axis, down)
        array = jnp.concatenate([before, array, after], axis=dim)
    return array


def smooth_fields(values, rows_factor, column_factor):
    left_done = jnp.einsum("ij,mjk->mik", rows_factor, values, precision=PRECISE)
    return jnp.einsum("mik,kl->mil", left_done, column_factor, precision=PRECISE)


def smooth_adjoint(values, rows_factor, column_factor):
    left_done = jnp.einsum("ji,mjk->mik", rows_factor, values, precision=PRECISE)
    return jnp.einsum("mik,lk->mil", left_done, column_factor, precision=PRECISE)


def interpolate(extended, refine):
    fraction = jnp.arange(refine, dtype=jnp.float32) / refine
    below_row = extended[..., :-1, None, :]
    above_row = extended[..., 1:, None, :]
    row_terms = below_row * (1.0 - fraction)[:, None] + above_row * fraction[:, None]
    dims_of = row_terms.shape
    row_terms = row_terms.reshape(dims_of[:-3] + (dims_of[-3] * refine, dims_of[-1]))
    wrapped = jnp.roll(row_terms, -1, axis=-1)
    col_terms = row_terms[..., None] * (1.0 - fraction) + wrapped[..., None] * fraction
    return col_terms.reshape(row_terms.shape[:-1] + (row_terms.shape[-1] * refine,))


def interpolate_adjoint(fine_field, refine):
    fraction = jnp.arange(refine, dtype=jnp.float32) / refine
    dims_of = fine_field.shape
    col_terms = fine_field.reshape(dims_of[:-1] + (dims_of[-1] // refine, refine))
    coarse_cols = jnp.sum(col_terms * (1.0 - fraction), axis=-1) + jnp.roll(
        jnp.sum(col_terms * fraction, axis=-1), 1, axis=-1
    )
    row_terms = coarse_cols.reshape(
        dims_of[:-2] + (dims_of[-2] // refine, refine, dims_of[-1] // refine)
    )
    below_part = jnp.sum(row_terms * (1.0 - fraction)[:, None], axis=-2)
    above_part = jnp.sum(row_terms * fraction[:, None], axis=-2)
    zero_row = jnp.zeros_like(below_part)
    return jnp.concatenate([below_part, zero_row], axis=-2) + jnp.concatenate(
        [zero_row, above_part], axis=-2
    )


def diffuse(values, diffusivity, fold_map):
    is_last = lax.axis_index("wide") == lax.axis_size("wide") - 1
    root_kappa = jnp.sqrt(diffusivity)
    for _ in range(STEPS):
        scaled = root_kappa * values
        padded = with_halo(scaled, (("wide", 1), ("lev", 0)), 1)
        folded = jnp.take(scaled[:, -1, :], fold_map, axis=1)
        padded = padded.at[1:-1, -1, :].set(jnp.where(is_last, folded, padded[1:-1, -1, :]))
        across = (
            padded[1:-1, 2:, :]
            + padded[1:-1, :-2, :]
            + jnp.roll(scaled, 1, axis=2)
            + jnp.roll(scaled, -1, axis=2)
            - 4.0 * scaled
        )
        vertical = padded[2:, 1:-1, :] + padded[:-2, 1:-1, :] - 2.0 * scaled
        values = values + root_kappa * (across + VERTICAL_WEIGHT * vertical)
    return values


def huber_weigh(increment, innovation, ocean_cells, huber_blocks):
    misfit = increment - innovation
    expanded = jnp.repeat(jnp.repeat(huber_blocks, REFINE, axis=1), REFINE, axis=2)
    weight = jnp.where(expanded == 1, HUBER_EDGE / jnp.maximum(jnp.abs(misfit), HUBER_EDGE), 1.0)
    return ocean_cells * weight * misfit


def on_device(
    member_control,
    static_control,
    perturbations,
    innovation,
    diffusivity,
    rows_factor,
    column_factor,
    ocean_mask,
    huber_blocks,
    fold_map,
):
    members = perturbations.shape[0]
    member_scale = (members - 1) ** (-0.5)
    wide_count = lax.axis_size("wide")
    smoothed = smooth_fields(member_control, rows_factor, column_factor)
    held, coarse_rows, width = smoothed.shape
    tile_rows = coarse_rows // wide_count
    main_rows = smoothed.reshape(held, wide_count, tile_rows, width)
    next_rows = jnp.concatenate([smoothed[:, tile_rows::tile_rows, :], smoothed[:, -1:, :]], axis=1)
    windows = jnp.concatenate([main_rows, next_rows[:, :, None, :]], axis=2)
    arrived = lax.all_to_all(windows, "wide", split_axis=1, concat_axis=0, tiled=True)
    extended = arrived.reshape(members, tile_rows + 1, width)
    fine_field = interpolate(extended, REFINE)
    ensemble = jnp.sum(fine_field[:, None] * perturbations, axis=0)
    ocean_cells = ocean_mask.astype(jnp.float32)
    increment = ocean_cells * (
        member_scale * ensemble + diffuse(static_control, diffusivity, fold_map)
    )
    weighted = huber_weigh(increment, innovation, ocean_cells, huber_blocks)
    static_gradient = static_control + diffuse(weighted, diffusivity, fold_map)
    fine_terms = jnp.sum(perturbations * weighted[None], axis=1) * member_scale
    level_part = interpolate_adjoint(fine_terms, REFINE)
    ext_grad = lax.psum(level_part, "lev")
    windows = lax.all_to_all(ext_grad[:, None], "wide", split_axis=0, concat_axis=1, tiled=True)
    main_rows = windows[:, :, :tile_rows, :]
    next_rows = windows[:, :, tile_rows, :]
    main_rows = main_rows.at[:, 1:, 0, :].add(next_rows[:, :-1, :])
    main_rows = main_rows.at[:, -1, tile_rows - 1, :].add(next_rows[:, -1, :])
    smooth_grad = main_rows.reshape(held, coarse_rows, width)
    member_gradient = member_control + smooth_adjoint(smooth_grad, rows_factor, column_factor)
    return (increment, member_gradient, static_gradient)


def solution(mesh):
    return jax.shard_map(
        on_device,
        mesh=mesh,
        in_specs=(
            P("wide", None, None),
            P("lev", "wide", None),
            P(None, "lev", "wide", None),
            P("lev", "wide", None),
            P("lev", "wide", None),
            P(),
            P(),
            P("wide", None),
            P("lev", "wide", None),
            P(),
        ),
        out_specs=(P("lev", "wide", None), P("wide", None, None), P("lev", "wide", None)),
        check_vma=False,
    )
```

profile of v0, /device:TPU:0, one launch (start us, length us, event | category | flops | bytes accessed | tf_op | source)
XLA Modules:
  0.0 148.4 jit_solution(14129248455665932806)
XLA Ops:
  4.0 3.0 %collective-permute-start = (f32[4,1,1024]{2,0,1:T(4,128)S(1)}, f32[4,1,1024]{2,0,1:T(4,128)S(1)}, u32[]{:S(2)}, u32[]{:S(2)}) collective-permute-start(f32[4,1,1024]{2,0,1:T(4,128)S(1)} %get-tuple-element.178), channel_id=1, source_target_pairs={{0,2},{2,4},{4,6},{6,8},{8,10},{10,12},{12,14},{14,16},{16,18},{18... | collective-permute-start | bytes 49160 | tf_op jit(solution)/shard_map/ppermute | solution.py:20
  8.7 8.0 %all-to-all-start = ((f32[1,16,2,128]{3,2,0,1:T(2,128)}), f32[1,16,2,128]{3,2,0,1:T(2,128)S(1)}, u32[]{:S(2)}, u32[]{:S(2)}) async-start(f32[1,16,2,128]{3,2,0,1:T(2,128)} %copy.546), calls=%async_computation | async-start | bytes 32768 | tf_op jit(solution)/shard_map/all_to_all | solution.py:114
  19.2 2.8 %gather_fusion = f32[1024,4]{1,0:T(8,128)S(1)} fusion(f32[4,1024]{0,1:T(8,128)S(1)} %copy.555, s32[1024]{0:T(1024)S(1)} %fusion.62), kind=kCustom, calls=%fused_computation.clone | custom fusion | bytes 36864 | tf_op jit(solution)/shard_map/jit(_take)/gather | solution.py:72
  23.6 3.4 %collective-permute-start.2 = (f32[1,10,1024]{2,0,1:T(1,128)S(1)}, f32[1,10,1024]{2,0,1:T(1,128)S(1)}, u32[]{:S(2)}, u32[]{:S(2)}) collective-permute-start(f32[1,10,1024]{2,0,1:T(1,128)S(1)} %get-tuple-element.135), channel_id=1, source_target_pairs={{0,1},{2,3},{4,5},{6,7},{8,9},{10,11},{12,13},{14,15},{16,17},{18,... | collective-permute-start | bytes 122888 | tf_op jit(solution)/shard_map/ppermute | solution.py:20
  31.9 2.9 %copy.552 = f32[16,8,1024]{2,1,0:T(8,128)S(1)} copy(f32[16,8,1024]{0,2,1:T(8,128)} %fusion.2) | data formatting | bytes 1048576 | tf_op jit(solution)/shard_map/add | solution.py:44
  37.2 3.0 %collective-permute-start.4 = (f32[4,1,1024]{2,0,1:T(4,128)S(1)}, f32[4,1,1024]{2,0,1:T(4,128)S(1)}, u32[]{:S(2)}, u32[]{:S(2)}) collective-permute-start(f32[4,1,1024]{2,0,1:T(4,128)S(1)} %get-tuple-element.171), channel_id=1, source_target_pairs={{0,2},{2,4},{4,6},{6,8},{8,10},{10,12},{12,14},{14,16},{16,18},{18... | collective-permute-start | bytes 49160 | tf_op jit(solution)/shard_map/ppermute | solution.py:20
  40.5 2.8 %gather_fusion.1 = f32[1024,4]{1,0:T(8,128)S(1)} fusion(f32[4,1024]{0,1:T(8,128)S(1)} %copy.563, s32[1024]{0:T(1024)S(1)} %fusion.62), kind=kCustom, calls=%fused_computation.1.clone | custom fusion | bytes 36864 | tf_op jit(solution)/shard_map/jit(_take)/gather | solution.py:72
  43.6 4.5 %collective-permute-start.6 = (f32[1,10,1024]{2,0,1:T(1,128)S(1)}, f32[1,10,1024]{2,0,1:T(1,128)S(1)}, u32[]{:S(2)}, u32[]{:S(2)}) collective-permute-start(f32[1,10,1024]{2,0,1:T(1,128)S(1)} %get-tuple-element.133), channel_id=1, source_target_pairs={{0,1},{2,3},{4,5},{6,7},{8,9},{10,11},{12,13},{14,15},{16,17},{18,... | collective-permute-start | bytes 122888 | tf_op jit(solution)/shard_map/ppermute | solution.py:20
  49.8 4.4 %collective-permute-done.7 = f32[1,10,1024]{2,0,1:T(1,128)S(1)} collective-permute-done((f32[1,10,1024]{2,0,1:T(1,128)S(1)}, f32[1,10,1024]{2,0,1:T(1,128)S(1)}, u32[]{:S(2)}, u32[]{:S(2)}) %collective-permute-start.7) | collective-permute-done | bytes 40992 | tf_op jit(solution)/shard_map/ppermute | solution.py:21
  56.3 3.0 %collective-permute-start.8 = (f32[4,1,1024]{2,0,1:T(4,128)S(1)}, f32[4,1,1024]{2,0,1:T(4,128)S(1)}, u32[]{:S(2)}, u32[]{:S(2)}) collective-permute-start(f32[4,1,1024]{2,0,1:T(4,128)S(1)} %get-tuple-element.164), channel_id=1, source_target_pairs={{0,2},{2,4},{4,6},{6,8},{8,10},{10,12},{12,14},{14,16},{16,18},{18... | collective-permute-start | bytes 49160 | tf_op jit(solution)/shard_map/ppermute | solution.py:20
  59.6 2.8 %gather_fusion.2 = f32[1024,4]{1,0:T(8,128)S(1)} fusion(f32[4,1024]{0,1:T(8,128)S(1)} %copy.570, s32[1024]{0:T(1024)S(1)} %fusion.62), kind=kCustom, calls=%fused_computation.2.clone | custom fusion | bytes 36864 | tf_op jit(solution)/shard_map/jit(_take)/gather | solution.py:72
  65.8 4.3 %collective-permute-done.11 = f32[1,10,1024]{2,0,1:T(1,128)S(1)} collective-permute-done((f32[1,10,1024]{2,0,1:T(1,128)S(1)}, f32[1,10,1024]{2,0,1:T(1,128)S(1)}, u32[]{:S(2)}, u32[]{:S(2)}) %collective-permute-start.11) | collective-permute-done | bytes 40992 | tf_op jit(solution)/shard_map/ppermute | solution.py:21
  72.3 2.8 %gather_fusion.3 = f32[1024,4]{1,0:T(8,128)S(1)} fusion(f32[4,1024]{0,1:T(8,128)S(1)} %copy.583, s32[1024]{0:T(1024)S(1)} %fusion.62), kind=kCustom, calls=%fused_computation.3.clone | custom fusion | bytes 36864 | tf_op jit(solution)/shard_map/jit(_take)/gather | solution.py:72
  76.6 3.0 %collective-permute-start.12 = (f32[4,1,1024]{2,0,1:T(4,128)S(1)}, f32[4,1,1024]{2,0,1:T(4,128)S(1)}, u32[]{:S(2)}, u32[]{:S(2)}) collective-permute-start(f32[4,1,1024]{2,0,1:T(4,128)S(1)} %get-tuple-element.157), channel_id=1, source_target_pairs={{0,2},{2,4},{4,6},{6,8},{8,10},{10,12},{12,14},{14,16},{16,18},{18... | collective-permute-start | bytes 49160 | tf_op jit(solution)/shard_map/ppermute | solution.py:20
  82.3 5.0 %fusion.1 = (f32[16,8,128]{0,2,1:T(8,128)S(1)}, f32[16,8,128]{0,2,1:T(8,128)S(1)}) fusion(f32[16,8,1024]{0,2,1:T(8,128)} %copy.577, f32[8]{0:T(128)S(1)} %get-tuple-element.185, f32[8]{0:T(128)S(1)} %get-tuple-element.186), kind=kLoop, calls=%fused_computation.9 | loop fusion | flops 491520 | bytes 655424 | tf_op jit(solution)/shard_map/reduce_sum | solution.py:53
  87.6 8.9 %psum.7 = f32[16,1,2,128]{0,3,2,1:T(8,128)S(1)} all-reduce(f32[16,1,2,128]{0,3,2,1:T(8,128)S(1)} %add_bitcast_fusion), channel_id=1, replica_groups=mesh['wide'=16,'lev'=2] {'lev'}, use_global_device_ids=true, to_apply=%region_6.8 | all-reduce | flops 4096 | bytes 32768 | tf_op jit(solution)/shard_map/psum | solution.py:126
  97.2 6.2 %all-to-all-start.1 = ((f32[16,1,2,128]{3,2,1,0:T(2,128)}), f32[16,1,2,128]{3,2,1,0:T(2,128)S(1)}, u32[]{:S(2)}, u32[]{:S(2)}) async-start(f32[16,1,2,128]{3,2,1,0:T(2,128)} %copy.578), calls=%async_computation.1 | async-start | bytes 32768 | tf_op jit(solution)/shard_map/all_to_all | solution.py:127
  103.6 3.9 %collective-permute-start.14 = (f32[1,10,1024]{2,0,1:T(1,128)S(1)}, f32[1,10,1024]{2,0,1:T(1,128)S(1)}, u32[]{:S(2)}, u32[]{:S(2)}) collective-permute-start(f32[1,10,1024]{2,0,1:T(1,128)S(1)} %get-tuple-element.129), channel_id=1, source_target_pairs={{0,1},{2,3},{4,5},{6,7},{8,9},{10,11},{12,13},{14,15},{16,17},{18,... | collective-permute-start | bytes 122888 | tf_op jit(solution)/shard_map/ppermute | solution.py:20
  115.7 3.0 %collective-permute-start.16 = (f32[4,1,1024]{2,0,1:T(4,128)S(1)}, f32[4,1,1024]{2,0,1:T(4,128)S(1)}, u32[]{:S(2)}, u32[]{:S(2)}) collective-permute-start(f32[4,1,1024]{2,0,1:T(4,128)S(1)} %get-tuple-element.150), channel_id=1, source_target_pairs={{0,2},{2,4},{4,6},{6,8},{8,10},{10,12},{12,14},{14,16},{16,18},{18... | collective-permute-start | bytes 49160 | tf_op jit(solution)/shard_map/ppermute | solution.py:20
  119.1 2.8 %gather_fusion.4 = f32[1024,4]{1,0:T(8,128)S(1)} fusion(f32[4,1024]{0,1:T(8,128)S(1)} %copy.592, s32[1024]{0:T(1024)S(1)} %fusion.62), kind=kCustom, calls=%fused_computation.4.clone | custom fusion | bytes 36864 | tf_op jit(solution)/shard_map/jit(_take)/gather | solution.py:72
  126.1 4.5 %collective-permute-done.19 = f32[1,10,1024]{2,0,1:T(1,128)S(1)} collective-permute-done((f32[1,10,1024]{2,0,1:T(1,128)S(1)}, f32[1,10,1024]{2,0,1:T(1,128)S(1)}, u32[]{:S(2)}, u32[]{:S(2)}) %collective-permute-start.19) | collective-permute-done | bytes 40992 | tf_op jit(solution)/shard_map/ppermute | solution.py:21
  132.8 3.0 %collective-permute-start.20 = (f32[4,1,1024]{2,0,1:T(4,128)S(1)}, f32[4,1,1024]{2,0,1:T(4,128)S(1)}, u32[]{:S(2)}, u32[]{:S(2)}) collective-permute-start(f32[4,1,1024]{2,0,1:T(4,128)S(1)} %get-tuple-element.143), channel_id=1, source_target_pairs={{0,2},{2,4},{4,6},{6,8},{8,10},{10,12},{12,14},{14,16},{16,18},{18... | collective-permute-start | bytes 49160 | tf_op jit(solution)/shard_map/ppermute | solution.py:20
  136.2 2.8 %gather_fusion.5 = f32[1024,4]{1,0:T(8,128)S(1)} fusion(f32[4,1024]{0,1:T(8,128)S(1)} %copy.603, s32[1024]{0:T(1024)S(1)} %fusion.62), kind=kCustom, calls=%fused_computation.5.clone | custom fusion | bytes 36864 | tf_op jit(solution)/shard_map/jit(_take)/gather | solution.py:72
  142.6 4.5 %collective-permute-done.23 = f32[1,10,1024]{2,0,1:T(1,128)S(1)} collective-permute-done((f32[1,10,1024]{2,0,1:T(1,128)S(1)}, f32[1,10,1024]{2,0,1:T(1,128)S(1)}, u32[]{:S(2)}, u32[]{:S(2)}) %collective-permute-start.23) | collective-permute-done | bytes 40992 | tf_op jit(solution)/shard_map/ppermute | solution.py:21
  (178 shorter events, 51.0 us)
Async XLA Ops:
  2.7 20.8 %collective-permute-start.1 = (f32[4,1,1024]{2,0,1:T(4,128)S(1)}, f32[4,1,1024]{2,0,1:T(4,128)S(1)}, u32[]{:S(2)}, u32[]{:S(2)}) collective-permute-start(f32[4,1,1024]{2,0,1:T(4,128)S(1)} %get-tuple-element.177), channel_id=1, source_target_pairs={{2,0},{4,2},{6,4},{8,6},{10,8},{12,10},{14,12},{16,14},{18,16},{20... | collective-permute-start | bytes 49160 | tf_op jit(solution)/shard_map/ppermute | solution.py:21
  4.0 19.5 %collective-permute-start = (f32[4,1,1024]{2,0,1:T(4,128)S(1)}, f32[4,1,1024]{2,0,1:T(4,128)S(1)}, u32[]{:S(2)}, u32[]{:S(2)}) collective-permute-start(f32[4,1,1024]{2,0,1:T(4,128)S(1)} %get-tuple-element.178), channel_id=1, source_target_pairs={{0,2},{2,4},{4,6},{6,8},{8,10},{10,12},{12,14},{14,16},{16,18},{18... | collective-permute-start | bytes 49160 | tf_op jit(solution)/shard_map/ppermute | solution.py:20
  8.7 19.7 %all-to-all-start = ((f32[1,16,2,128]{3,2,0,1:T(2,128)}), f32[1,16,2,128]{3,2,0,1:T(2,128)S(1)}, u32[]{:S(2)}, u32[]{:S(2)}) async-start(f32[1,16,2,128]{3,2,0,1:T(2,128)} %copy.546), calls=%async_computation | async-start | bytes 32768 | tf_op jit(solution)/shard_map/all_to_all | solution.py:114
  23.6 11.4 %collective-permute-start.2 = (f32[1,10,1024]{2,0,1:T(1,128)S(1)}, f32[1,10,1024]{2,0,1:T(1,128)S(1)}, u32[]{:S(2)}, u32[]{:S(2)}) collective-permute-start(f32[1,10,1024]{2,0,1:T(1,128)S(1)} %get-tuple-element.135), channel_id=1, source_target_pairs={{0,1},{2,3},{4,5},{6,7},{8,9},{10,11},{12,13},{14,15},{16,17},{18,... | collective-permute-start | bytes 122888 | tf_op jit(solution)/shard_map/ppermute | solution.py:20
  27.1 8.0 %collective-permute-start.3 = (f32[1,10,1024]{2,0,1:T(1,128)S(1)}, f32[1,10,1024]{2,0,1:T(1,128)S(1)}, u32[]{:S(2)}, u32[]{:S(2)}) collective-permute-start(f32[1,10,1024]{2,0,1:T(1,128)S(1)} %get-tuple-element.136), channel_id=1, source_target_pairs={{1,0},{3,2},{5,4},{7,6},{9,8},{11,10},{13,12},{15,14},{17,16},{19,... | collective-permute-start | bytes 122888 | tf_op jit(solution)/shard_map/ppermute | solution.py:21
  35.9 7.7 %collective-permute-start.5 = (f32[4,1,1024]{2,0,1:T(4,128)S(1)}, f32[4,1,1024]{2,0,1:T(4,128)S(1)}, u32[]{:S(2)}, u32[]{:S(2)}) collective-permute-start(f32[4,1,1024]{2,0,1:T(4,128)S(1)} %get-tuple-element.170), channel_id=1, source_target_pairs={{2,0},{4,2},{6,4},{8,6},{10,8},{12,10},{14,12},{16,14},{18,16},{20... | collective-permute-start | bytes 49160 | tf_op jit(solution)/shard_map/ppermute | solution.py:21
  37.2 6.4 %collective-permute-start.4 = (f32[4,1,1024]{2,0,1:T(4,128)S(1)}, f32[4,1,1024]{2,0,1:T(4,128)S(1)}, u32[]{:S(2)}, u32[]{:S(2)}) collective-permute-start(f32[4,1,1024]{2,0,1:T(4,128)S(1)} %get-tuple-element.171), channel_id=1, source_target_pairs={{0,2},{2,4},{4,6},{6,8},{8,10},{10,12},{12,14},{14,16},{16,18},{18... | collective-permute-start | bytes 49160 | tf_op jit(solution)/shard_map/ppermute | solution.py:20
  43.6 6.2 %collective-permute-start.6 = (f32[1,10,1024]{2,0,1:T(1,128)S(1)}, f32[1,10,1024]{2,0,1:T(1,128)S(1)}, u32[]{:S(2)}, u32[]{:S(2)}) collective-permute-start(f32[1,10,1024]{2,0,1:T(1,128)S(1)} %get-tuple-element.133), channel_id=1, source_target_pairs={{0,1},{2,3},{4,5},{6,7},{8,9},{10,11},{12,13},{14,15},{16,17},{18,... | collective-permute-start | bytes 122888 | tf_op jit(solution)/shard_map/ppermute | solution.py:20
  48.2 6.0 %collective-permute-start.7 = (f32[1,10,1024]{2,0,1:T(1,128)S(1)}, f32[1,10,1024]{2,0,1:T(1,128)S(1)}, u32[]{:S(2)}, u32[]{:S(2)}) collective-permute-start(f32[1,10,1024]{2,0,1:T(1,128)S(1)} %get-tuple-element.134), channel_id=1, source_target_pairs={{1,0},{3,2},{5,4},{7,6},{9,8},{11,10},{13,12},{15,14},{17,16},{19,... | collective-permute-start | bytes 122888 | tf_op jit(solution)/shard_map/ppermute | solution.py:21
  55.0 7.7 %collective-permute-start.9 = (f32[4,1,1024]{2,0,1:T(4,128)S(1)}, f32[4,1,1024]{2,0,1:T(4,128)S(1)}, u32[]{:S(2)}, u32[]{:S(2)}) collective-permute-start(f32[4,1,1024]{2,0,1:T(4,128)S(1)} %get-tuple-element.163), channel_id=1, source_target_pairs={{2,0},{4,2},{6,4},{8,6},{10,8},{12,10},{14,12},{16,14},{18,16},{20... | collective-permute-start | bytes 49160 | tf_op jit(solution)/shard_map/ppermute | solution.py:21
  56.3 6.4 %collective-permute-start.8 = (f32[4,1,1024]{2,0,1:T(4,128)S(1)}, f32[4,1,1024]{2,0,1:T(4,128)S(1)}, u32[]{:S(2)}, u32[]{:S(2)}) collective-permute-start(f32[4,1,1024]{2,0,1:T(4,128)S(1)} %get-tuple-element.164), channel_id=1, source_target_pairs={{0,2},{2,4},{4,6},{6,8},{8,10},{10,12},{12,14},{14,16},{16,18},{18... | collective-permute-start | bytes 49160 | tf_op jit(solution)/shard_map/ppermute | solution.py:20
  64.2 5.9 %collective-permute-start.11 = (f32[1,10,1024]{2,0,1:T(1,128)S(1)}, f32[1,10,1024]{2,0,1:T(1,128)S(1)}, u32[]{:S(2)}, u32[]{:S(2)}) collective-permute-start(f32[1,10,1024]{2,0,1:T(1,128)S(1)} %get-tuple-element.132), channel_id=1, source_target_pairs={{1,0},{3,2},{5,4},{7,6},{9,8},{11,10},{13,12},{15,14},{17,16},{19,... | collective-permute-start | bytes 122888 | tf_op jit(solution)/shard_map/ppermute | solution.py:21
  75.3 28.1 %collective-permute-start.13 = (f32[4,1,1024]{2,0,1:T(4,128)S(1)}, f32[4,1,1024]{2,0,1:T(4,128)S(1)}, u32[]{:S(2)}, u32[]{:S(2)}) collective-permute-start(f32[4,1,1024]{2,0,1:T(4,128)S(1)} %get-tuple-element.156), channel_id=1, source_target_pairs={{2,0},{4,2},{6,4},{8,6},{10,8},{12,10},{14,12},{16,14},{18,16},{20... | collective-permute-start | bytes 49160 | tf_op jit(solution)/shard_map/ppermute | solution.py:21
  76.6 26.8 %collective-permute-start.12 = (f32[4,1,1024]{2,0,1:T(4,128)S(1)}, f32[4,1,1024]{2,0,1:T(4,128)S(1)}, u32[]{:S(2)}, u32[]{:S(2)}) collective-permute-start(f32[4,1,1024]{2,0,1:T(4,128)S(1)} %get-tuple-element.157), channel_id=1, source_target_pairs={{0,2},{2,4},{4,6},{6,8},{8,10},{10,12},{12,14},{14,16},{16,18},{18... | collective-permute-start | bytes 49160 | tf_op jit(solution)/shard_map/ppermute | solution.py:20
  97.2 12.7 %all-to-all-start.1 = ((f32[16,1,2,128]{3,2,1,0:T(2,128)}), f32[16,1,2,128]{3,2,1,0:T(2,128)S(1)}, u32[]{:S(2)}, u32[]{:S(2)}) async-start(f32[16,1,2,128]{3,2,1,0:T(2,128)} %copy.578), calls=%async_computation.1 | async-start | bytes 32768 | tf_op jit(solution)/shard_map/all_to_all | solution.py:127
  103.6 7.9 %collective-permute-start.14 = (f32[1,10,1024]{2,0,1:T(1,128)S(1)}, f32[1,10,1024]{2,0,1:T(1,128)S(1)}, u32[]{:S(2)}, u32[]{:S(2)}) collective-permute-start(f32[1,10,1024]{2,0,1:T(1,128)S(1)} %get-tuple-element.129), channel_id=1, source_target_pairs={{0,1},{2,3},{4,5},{6,7},{8,9},{10,11},{12,13},{14,15},{16,17},{18,... | collective-permute-start | bytes 122888 | tf_op jit(solution)/shard_map/ppermute | solution.py:20
  107.5 5.9 %collective-permute-start.15 = (f32[1,10,1024]{2,0,1:T(1,128)S(1)}, f32[1,10,1024]{2,0,1:T(1,128)S(1)}, u32[]{:S(2)}, u32[]{:S(2)}) collective-permute-start(f32[1,10,1024]{2,0,1:T(1,128)S(1)} %get-tuple-element.130), channel_id=1, source_target_pairs={{1,0},{3,2},{5,4},{7,6},{9,8},{11,10},{13,12},{15,14},{17,16},{19,... | collective-permute-start | bytes 122888 | tf_op jit(solution)/shard_map/ppermute | solution.py:21
  114.4 7.9 %collective-permute-start.17 = (f32[4,1,1024]{2,0,1:T(4,128)S(1)}, f32[4,1,1024]{2,0,1:T(4,128)S(1)}, u32[]{:S(2)}, u32[]{:S(2)}) collective-permute-start(f32[4,1,1024]{2,0,1:T(4,128)S(1)} %get-tuple-element.149), channel_id=1, source_target_pairs={{2,0},{4,2},{6,4},{8,6},{10,8},{12,10},{14,12},{16,14},{18,16},{20... | collective-permute-start | bytes 49160 | tf_op jit(solution)/shard_map/ppermute | solution.py:21
  115.7 6.6 %collective-permute-start.16 = (f32[4,1,1024]{2,0,1:T(4,128)S(1)}, f32[4,1,1024]{2,0,1:T(4,128)S(1)}, u32[]{:S(2)}, u32[]{:S(2)}) collective-permute-start(f32[4,1,1024]{2,0,1:T(4,128)S(1)} %get-tuple-element.150), channel_id=1, source_target_pairs={{0,2},{2,4},{4,6},{6,8},{8,10},{10,12},{12,14},{14,16},{16,18},{18... | collective-permute-start | bytes 49160 | tf_op jit(solution)/shard_map/ppermute | solution.py:20
  122.4 3.7 %collective-permute-start.18 = (f32[1,10,1024]{2,0,1:T(1,128)S(1)}, f32[1,10,1024]{2,0,1:T(1,128)S(1)}, u32[]{:S(2)}, u32[]{:S(2)}) collective-permute-start(f32[1,10,1024]{2,0,1:T(1,128)S(1)} %get-tuple-element.127), channel_id=1, source_target_pairs={{0,1},{2,3},{4,5},{6,7},{8,9},{10,11},{12,13},{14,15},{16,17},{18,... | collective-permute-start | bytes 122888 | tf_op jit(solution)/shard_map/ppermute | solution.py:20
  124.4 6.3 %collective-permute-start.19 = (f32[1,10,1024]{2,0,1:T(1,128)S(1)}, f32[1,10,1024]{2,0,1:T(1,128)S(1)}, u32[]{:S(2)}, u32[]{:S(2)}) collective-permute-start(f32[1,10,1024]{2,0,1:T(1,128)S(1)} %get-tuple-element.128), channel_id=1, source_target_pairs={{1,0},{3,2},{5,4},{7,6},{9,8},{11,10},{13,12},{15,14},{17,16},{19,... | collective-permute-start | bytes 122888 | tf_op jit(solution)/shard_map/ppermute | solution.py:21
  131.5 7.9 %collective-permute-start.21 = (f32[4,1,1024]{2,0,1:T(4,128)S(1)}, f32[4,1,1024]{2,0,1:T(4,128)S(1)}, u32[]{:S(2)}, u32[]{:S(2)}) collective-permute-start(f32[4,1,1024]{2,0,1:T(4,128)S(1)} %get-tuple-element.142), channel_id=1, source_target_pairs={{2,0},{4,2},{6,4},{8,6},{10,8},{12,10},{14,12},{16,14},{18,16},{20... | collective-permute-start | bytes 49160 | tf_op jit(solution)/shard_map/ppermute | solution.py:21
  132.8 6.6 %collective-permute-start.20 = (f32[4,1,1024]{2,0,1:T(4,128)S(1)}, f32[4,1,1024]{2,0,1:T(4,128)S(1)}, u32[]{:S(2)}, u32[]{:S(2)}) collective-permute-start(f32[4,1,1024]{2,0,1:T(4,128)S(1)} %get-tuple-element.143), channel_id=1, source_target_pairs={{0,2},{2,4},{4,6},{6,8},{8,10},{10,12},{12,14},{14,16},{16,18},{18... | collective-permute-start | bytes 49160 | tf_op jit(solution)/shard_map/ppermute | solution.py:20
  140.9 6.2 %collective-permute-start.23 = (f32[1,10,1024]{2,0,1:T(1,128)S(1)}, f32[1,10,1024]{2,0,1:T(1,128)S(1)}, u32[]{:S(2)}, u32[]{:S(2)}) collective-permute-start(f32[1,10,1024]{2,0,1:T(1,128)S(1)} %get-tuple-element.126), channel_id=1, source_target_pairs={{1,0},{3,2},{5,4},{7,6},{9,8},{11,10},{13,12},{15,14},{17,16},{19,... | collective-permute-start | bytes 122888 | tf_op jit(solution)/shard_map/ppermute | solution.py:21
  (9 other events, 157.2 us)
where the time goes:
time: 149 us; the launch traced here: 148 us
  starting transfers between devices  64.7 us (43%)
  local copies, waits for them, and re-layouts  32 us (21%)
  waiting for transfers between devices  22.2 us (15%)
  other arithmetic  16.8 us (11%)
  blocking collectives  8.93 us (6%)
  matrix products  2.02 us (1%)
  between operations  1.71 us (1%)
    ppermute x12, starting transfers between devices, with_halo(): before = lax.ppermute(last, axis, up)  35 us
    ppermute x12, waiting for transfers between devices, with_halo(): after = lax.ppermute(first, axis, down)  19.7 us
    gather x12, local copies, waits for them, and re-layouts, diffuse(): folded = jnp.take(scaled[:, -1, :], fold_map, axis=1)  18 us
    ppermute x12, starting transfers between devices, with_halo(): after = lax.ppermute(first, axis, down)  15.5 us
    psum x1, blocking collectives, on_device(): ext_grad = lax.psum(level_part, 'lev')  8.93 us
    all_to_all x1, starting transfers between devices, on_device(): lax.all_to_all(windows, 'wide', split_axis=1, concat_axis=0, tiled=True)  7.95 us
    all_to_all x1, starting transfers between devices, on_device(): lax.all_to_all(ext_grad[:, None], 'wide', split_axis=0, concat_axis=1, ti...  6.24 us
    reduce_sum x1, other arithmetic, interpolate_adjoint(): jnp.sum(col_terms * fraction, axis=-1)  5.03 us
  transfers between devices with their start and end apart: 26, of which 10 were waited for; matrix products, arithmetic and copies ran while one was open for 26% of the time, Pallas kernels for 0%

commit v1 on v0

--- a/solution.py
+++ b/solution.py
@@ -123,7 +123,7 @@
     static_gradient = static_control + diffuse(weighted, diffusivity, fold_map)
     fine_terms = jnp.sum(perturbations * weighted[None], axis=1) * member_scale
     level_part = interpolate_adjoint(fine_terms, REFINE)
-    ext_grad = lax.psum(level_part, "lev")
+    ext_grad = jnp.sum(lax.all_gather(level_part, "lev"), axis=0)
     windows = lax.all_to_all(ext_grad[:, None], "wide", split_axis=0, concat_axis=1, tiled=True)
     main_rows = windows[:, :, :tile_rows, :]
     next_rows = windows[:, :, tile_rows, :]

time: 149 us -> 144 us (0.966)
  blocking collectives: 8.93 us -> 4.41 us
    psum x1 -> x0, blocking collectives: 8.93 us -> none  [on_device(): ext_grad = lax.psum(level_part, 'lev')]
    all_gather x0 -> x1, blocking collectives: none -> 4.41 us  [on_device(): ext_grad = jnp.sum(lax.all_gather(level_part, 'lev'), axis=0)]
    ppermute x12, waiting for transfers between devices: 19.7 us -> 17.9 us  [with_halo(): after = lax.ppermute(first, axis, down)]
    all_to_all x1, waiting for transfers between devices: 1.16 us -> 2.9 us  [on_device(): lax.all_to_all(ext_grad[:, None], 'wide', split_axis=0, concat_axis=1, ti...]
    ppermute x12, starting transfers between devices: 35 us -> 33.2 us  [with_halo(): before = lax.ppermute(last, axis, up)]
  transfers between devices with their start and end apart: 26 -> 26, of which waited for: 10 -> 10; matrix products, arithmetic and copies ran while one was open for 26% -> 29% of each run, Pallas kernels for 0% -> 0%
where the time goes in v1:
time: 144 us; the launch traced here: 143 us
  starting transfers between devices  63.6 us (44%)
  local copies, waits for them, and re-layouts  32 us (22%)
  waiting for transfers between devices  22.2 us (15%)
  other arithmetic  16.9 us (12%)
  blocking collectives  4.41 us (3%)
  matrix products  2.02 us (1%)
  between operations  1.71 us (1%)
    ppermute x12, starting transfers between devices, with_halo(): before = lax.ppermute(last, axis, up)  33.2 us
    gather x12, local copies, waits for them, and re-layouts, diffuse(): folded = jnp.take(scaled[:, -1, :], fold_map, axis=1)  18 us
    ppermute x12, waiting for transfers between devices, with_halo(): after = lax.ppermute(first, axis, down)  17.9 us
    ppermute x12, starting transfers between devices, with_halo(): after = lax.ppermute(first, axis, down)  15.5 us
    all_to_all x1, starting transfers between devices, on_device(): lax.all_to_all(windows, 'wide', split_axis=1, concat_axis=0, tiled=True)  7.95 us
    all_to_all x1, starting transfers between devices, on_device(): lax.all_to_all(ext_grad[:, None], 'wide', split_axis=0, concat_axis=1, ti...  6.93 us
    reduce_sum x1, other arithmetic, interpolate_adjoint(): jnp.sum(col_terms * fraction, axis=-1)  5.03 us
    all_gather x1, blocking collectives, on_device(): ext_grad = jnp.sum(lax.all_gather(level_part, 'lev'), axis=0)  4.41 us
  transfers between devices with their start and end apart: 26, of which 10 were waited for; matrix products, arithmetic and copies ran while one was open for 29% of the time, Pallas kernels for 0%

profile of v1, /device:TPU:0, one launch (start us, length us, event | category | flops | bytes accessed | tf_op | source)
XLA Modules:
  0.0 142.9 jit_solution(11908295344961641848)
XLA Ops:
  4.0 3.0 %collective-permute-start = (f32[4,1,1024]{2,0,1:T(4,128)S(1)}, f32[4,1,1024]{2,0,1:T(4,128)S(1)}, u32[]{:S(2)}, u32[]{:S(2)}) collective-permute-start(f32[4,1,1024]{2,0,1:T(4,128)S(1)} %get-tuple-element.181), channel_id=1, source_target_pairs={{0,2},{2,4},{4,6},{6,8},{8,10},{10,12},{12,14},{14,16},{16,18},{18... | collective-permute-start | bytes 49160 | tf_op jit(solution)/shard_map/ppermute | solution.py:20
  8.7 8.0 %all-to-all-start = ((f32[1,16,2,128]{3,2,0,1:T(2,128)}), f32[1,16,2,128]{3,2,0,1:T(2,128)S(1)}, u32[]{:S(2)}, u32[]{:S(2)}) async-start(f32[1,16,2,128]{3,2,0,1:T(2,128)} %copy.656), calls=%async_computation | async-start | bytes 32768 | tf_op jit(solution)/shard_map/all_to_all | solution.py:114
  19.2 2.8 %gather_fusion = f32[1024,4]{1,0:T(8,128)S(1)} fusion(f32[4,1024]{0,1:T(8,128)S(1)} %copy.665, s32[1024]{0:T(1024)S(1)} %fusion.62), kind=kCustom, calls=%fused_computation.clone | custom fusion | bytes 36864 | tf_op jit(solution)/shard_map/jit(_take)/gather | solution.py:72
  23.6 3.4 %collective-permute-start.2 = (f32[1,10,1024]{2,0,1:T(1,128)S(1)}, f32[1,10,1024]{2,0,1:T(1,128)S(1)}, u32[]{:S(2)}, u32[]{:S(2)}) collective-permute-start(f32[1,10,1024]{2,0,1:T(1,128)S(1)} %get-tuple-element.138), channel_id=1, source_target_pairs={{0,1},{2,3},{4,5},{6,7},{8,9},{10,11},{12,13},{14,15},{16,17},{18,... | collective-permute-start | bytes 122888 | tf_op jit(solution)/shard_map/ppermute | solution.py:20
  31.9 2.9 %copy.662 = f32[16,8,1024]{2,1,0:T(8,128)S(1)} copy(f32[16,8,1024]{0,2,1:T(8,128)} %fusion.2) | data formatting | bytes 1048576 | tf_op jit(solution)/shard_map/add | solution.py:44
  37.2 3.0 %collective-permute-start.4 = (f32[4,1,1024]{2,0,1:T(4,128)S(1)}, f32[4,1,1024]{2,0,1:T(4,128)S(1)}, u32[]{:S(2)}, u32[]{:S(2)}) collective-permute-start(f32[4,1,1024]{2,0,1:T(4,128)S(1)} %get-tuple-element.174), channel_id=1, source_target_pairs={{0,2},{2,4},{4,6},{6,8},{8,10},{10,12},{12,14},{14,16},{16,18},{18... | collective-permute-start | bytes 49160 | tf_op jit(solution)/shard_map/ppermute | solution.py:20
  40.5 2.8 %gather_fusion.1 = f32[1024,4]{1,0:T(8,128)S(1)} fusion(f32[4,1024]{0,1:T(8,128)S(1)} %copy.673, s32[1024]{0:T(1024)S(1)} %fusion.62), kind=kCustom, calls=%fused_computation.1.clone | custom fusion | bytes 36864 | tf_op jit(solution)/shard_map/jit(_take)/gather | solution.py:72
  43.6 4.5 %collective-permute-start.6 = (f32[1,10,1024]{2,0,1:T(1,128)S(1)}, f32[1,10,1024]{2,0,1:T(1,128)S(1)}, u32[]{:S(2)}, u32[]{:S(2)}) collective-permute-start(f32[1,10,1024]{2,0,1:T(1,128)S(1)} %get-tuple-element.136), channel_id=1, source_target_pairs={{0,1},{2,3},{4,5},{6,7},{8,9},{10,11},{12,13},{14,15},{16,17},{18,... | collective-permute-start | bytes 122888 | tf_op jit(solution)/shard_map/ppermute | solution.py:20
  49.8 4.4 %collective-permute-done.7 = f32[1,10,1024]{2,0,1:T(1,128)S(1)} collective-permute-done((f32[1,10,1024]{2,0,1:T(1,128)S(1)}, f32[1,10,1024]{2,0,1:T(1,128)S(1)}, u32[]{:S(2)}, u32[]{:S(2)}) %collective-permute-start.7) | collective-permute-done | bytes 40992 | tf_op jit(solution)/shard_map/ppermute | solution.py:21
  56.3 3.0 %collective-permute-start.8 = (f32[4,1,1024]{2,0,1:T(4,128)S(1)}, f32[4,1,1024]{2,0,1:T(4,128)S(1)}, u32[]{:S(2)}, u32[]{:S(2)}) collective-permute-start(f32[4,1,1024]{2,0,1:T(4,128)S(1)} %get-tuple-element.167), channel_id=1, source_target_pairs={{0,2},{2,4},{4,6},{6,8},{8,10},{10,12},{12,14},{14,16},{16,18},{18... | collective-permute-start | bytes 49160 | tf_op jit(solution)/shard_map/ppermute | solution.py:20
  59.6 2.8 %gather_fusion.2 = f32[1024,4]{1,0:T(8,128)S(1)} fusion(f32[4,1024]{0,1:T(8,128)S(1)} %copy.680, s32[1024]{0:T(1024)S(1)} %fusion.62), kind=kCustom, calls=%fused_computation.2.clone | custom fusion | bytes 36864 | tf_op jit(solution)/shard_map/jit(_take)/gather | solution.py:72
  65.8 4.3 %collective-permute-done.11 = f32[1,10,1024]{2,0,1:T(1,128)S(1)} collective-permute-done((f32[1,10,1024]{2,0,1:T(1,128)S(1)}, f32[1,10,1024]{2,0,1:T(1,128)S(1)}, u32[]{:S(2)}, u32[]{:S(2)}) %collective-permute-start.11) | collective-permute-done | bytes 40992 | tf_op jit(solution)/shard_map/ppermute | solution.py:21
  73.4 3.0 %collective-permute-start.12 = (f32[4,1,1024]{2,0,1:T(4,128)S(1)}, f32[4,1,1024]{2,0,1:T(4,128)S(1)}, u32[]{:S(2)}, u32[]{:S(2)}) collective-permute-start(f32[4,1,1024]{2,0,1:T(4,128)S(1)} %get-tuple-element.160), channel_id=1, source_target_pairs={{0,2},{2,4},{4,6},{6,8},{8,10},{10,12},{12,14},{14,16},{16,18},{18... | collective-permute-start | bytes 49160 | tf_op jit(solution)/shard_map/ppermute | solution.py:20
  79.1 5.0 %fusion.1 = (f32[16,8,128]{0,2,1:T(8,128)S(1)}, f32[16,8,128]{0,2,1:T(8,128)S(1)}) fusion(f32[16,8,1024]{0,2,1:T(8,128)} %copy.687, f32[8]{0:T(128)S(1)} %get-tuple-element.188, f32[8]{0:T(128)S(1)} %get-tuple-element.189), kind=kLoop, calls=%fused_computation.9 | loop fusion | flops 491520 | bytes 655424 | tf_op jit(solution)/shard_map/reduce_sum | solution.py:53
  84.6 2.8 %gather_fusion.3 = f32[1024,4]{1,0:T(8,128)S(1)} fusion(f32[4,1024]{0,1:T(8,128)S(1)} %copy.695, s32[1024]{0:T(1024)S(1)} %fusion.62), kind=kCustom, calls=%fused_computation.3.clone | custom fusion | bytes 36864 | tf_op jit(solution)/shard_map/jit(_take)/gather | solution.py:72
  87.7 4.4 %all-gather = f32[32,2,128]{2,1,0:T(2,128)S(1)} all-gather(f32[16,2,128]{2,1,0:T(2,128)S(1)} %copy.688), channel_id=2, replica_groups=mesh['wide'=16,'lev'=2] {'lev'}, dimensions={0}, use_global_device_ids=true | all-gather | bytes 49152 | tf_op jit(solution)/shard_map/all_gather | solution.py:126
  92.7 6.9 %all-to-all-start.1 = ((f32[16,1,2,128]{3,2,1,0:T(2,128)}), f32[16,1,2,128]{3,2,1,0:T(2,128)S(1)}, u32[]{:S(2)}, u32[]{:S(2)}) async-start(f32[16,1,2,128]{3,2,1,0:T(2,128)} %copy.690), calls=%async_computation.1 | async-start | bytes 32768 | tf_op jit(solution)/shard_map/all_to_all | solution.py:127
  103.3 2.9 %all-to-all-done.1 = f32[16,1,2,128]{3,2,1,0:T(2,128)S(1)} async-done(((f32[16,1,2,128]{3,2,1,0:T(2,128)}), f32[16,1,2,128]{3,2,1,0:T(2,128)S(1)}, u32[]{:S(2)}, u32[]{:S(2)}) %all-to-all-start.1) | async-done | bytes 16416 | tf_op jit(solution)/shard_map/all_to_all | solution.py:127
  110.2 3.0 %collective-permute-start.16 = (f32[4,1,1024]{2,0,1:T(4,128)S(1)}, f32[4,1,1024]{2,0,1:T(4,128)S(1)}, u32[]{:S(2)}, u32[]{:S(2)}) collective-permute-start(f32[4,1,1024]{2,0,1:T(4,128)S(1)} %get-tuple-element.153), channel_id=1, source_target_pairs={{0,2},{2,4},{4,6},{6,8},{8,10},{10,12},{12,14},{14,16},{16,18},{18... | collective-permute-start | bytes 49160 | tf_op jit(solution)/shard_map/ppermute | solution.py:20
  113.5 2.8 %gather_fusion.4 = f32[1024,4]{1,0:T(8,128)S(1)} fusion(f32[4,1024]{0,1:T(8,128)S(1)} %copy.704, s32[1024]{0:T(1024)S(1)} %fusion.62), kind=kCustom, calls=%fused_computation.4.clone | custom fusion | bytes 36864 | tf_op jit(solution)/shard_map/jit(_take)/gather | solution.py:72
  120.6 4.5 %collective-permute-done.19 = f32[1,10,1024]{2,0,1:T(1,128)S(1)} collective-permute-done((f32[1,10,1024]{2,0,1:T(1,128)S(1)}, f32[1,10,1024]{2,0,1:T(1,128)S(1)}, u32[]{:S(2)}, u32[]{:S(2)}) %collective-permute-start.19) | collective-permute-done | bytes 40992 | tf_op jit(solution)/shard_map/ppermute | solution.py:21
  127.3 3.0 %collective-permute-start.20 = (f32[4,1,1024]{2,0,1:T(4,128)S(1)}, f32[4,1,1024]{2,0,1:T(4,128)S(1)}, u32[]{:S(2)}, u32[]{:S(2)}) collective-permute-start(f32[4,1,1024]{2,0,1:T(4,128)S(1)} %get-tuple-element.146), channel_id=1, source_target_pairs={{0,2},{2,4},{4,6},{6,8},{8,10},{10,12},{12,14},{14,16},{16,18},{18... | collective-permute-start | bytes 49160 | tf_op jit(solution)/shard_map/ppermute | solution.py:20
  130.6 2.8 %gather_fusion.5 = f32[1024,4]{1,0:T(8,128)S(1)} fusion(f32[4,1024]{0,1:T(8,128)S(1)} %copy.715, s32[1024]{0:T(1024)S(1)} %fusion.62), kind=kCustom, calls=%fused_computation.5.clone | custom fusion | bytes 36864 | tf_op jit(solution)/shard_map/jit(_take)/gather | solution.py:72
  137.1 4.5 %collective-permute-done.23 = f32[1,10,1024]{2,0,1:T(1,128)S(1)} collective-permute-done((f32[1,10,1024]{2,0,1:T(1,128)S(1)}, f32[1,10,1024]{2,0,1:T(1,128)S(1)}, u32[]{:S(2)}, u32[]{:S(2)}) %collective-permute-start.23) | collective-permute-done | bytes 40992 | tf_op jit(solution)/shard_map/ppermute | solution.py:21
  (181 shorter events, 50.3 us)
Async XLA Ops:
  2.7 20.8 %collective-permute-start.1 = (f32[4,1,1024]{2,0,1:T(4,128)S(1)}, f32[4,1,1024]{2,0,1:T(4,128)S(1)}, u32[]{:S(2)}, u32[]{:S(2)}) collective-permute-start(f32[4,1,1024]{2,0,1:T(4,128)S(1)} %get-tuple-element.180), channel_id=1, source_target_pairs={{2,0},{4,2},{6,4},{8,6},{10,8},{12,10},{14,12},{16,14},{18,16},{20... | collective-permute-start | bytes 49160 | tf_op jit(solution)/shard_map/ppermute | solution.py:21
  4.0 19.5 %collective-permute-start = (f32[4,1,1024]{2,0,1:T(4,128)S(1)}, f32[4,1,1024]{2,0,1:T(4,128)S(1)}, u32[]{:S(2)}, u32[]{:S(2)}) collective-permute-start(f32[4,1,1024]{2,0,1:T(4,128)S(1)} %get-tuple-element.181), channel_id=1, source_target_pairs={{0,2},{2,4},{4,6},{6,8},{8,10},{10,12},{12,14},{14,16},{16,18},{18... | collective-permute-start | bytes 49160 | tf_op jit(solution)/shard_map/ppermute | solution.py:20
  8.7 19.7 %all-to-all-start = ((f32[1,16,2,128]{3,2,0,1:T(2,128)}), f32[1,16,2,128]{3,2,0,1:T(2,128)S(1)}, u32[]{:S(2)}, u32[]{:S(2)}) async-start(f32[1,16,2,128]{3,2,0,1:T(2,128)} %copy.656), calls=%async_computation | async-start | bytes 32768 | tf_op jit(solution)/shard_map/all_to_all | solution.py:114
  23.6 11.4 %collective-permute-start.2 = (f32[1,10,1024]{2,0,1:T(1,128)S(1)}, f32[1,10,1024]{2,0,1:T(1,128)S(1)}, u32[]{:S(2)}, u32[]{:S(2)}) collective-permute-start(f32[1,10,1024]{2,0,1:T(1,128)S(1)} %get-tuple-element.138), channel_id=1, source_target_pairs={{0,1},{2,3},{4,5},{6,7},{8,9},{10,11},{12,13},{14,15},{16,17},{18,... | collective-permute-start | bytes 122888 | tf_op jit(solution)/shard_map/ppermute | solution.py:20
  27.1 8.0 %collective-permute-start.3 = (f32[1,10,1024]{2,0,1:T(1,128)S(1)}, f32[1,10,1024]{2,0,1:T(1,128)S(1)}, u32[]{:S(2)}, u32[]{:S(2)}) collective-permute-start(f32[1,10,1024]{2,0,1:T(1,128)S(1)} %get-tuple-element.139), channel_id=1, source_target_pairs={{1,0},{3,2},{5,4},{7,6},{9,8},{11,10},{13,12},{15,14},{17,16},{19,... | collective-permute-start | bytes 122888 | tf_op jit(solution)/shard_map/ppermute | solution.py:21
  35.9 7.7 %collective-permute-start.5 = (f32[4,1,1024]{2,0,1:T(4,128)S(1)}, f32[4,1,1024]{2,0,1:T(4,128)S(1)}, u32[]{:S(2)}, u32[]{:S(2)}) collective-permute-start(f32[4,1,1024]{2,0,1:T(4,128)S(1)} %get-tuple-element.173), channel_id=1, source_target_pairs={{2,0},{4,2},{6,4},{8,6},{10,8},{12,10},{14,12},{16,14},{18,16},{20... | collective-permute-start | bytes 49160 | tf_op jit(solution)/shard_map/ppermute | solution.py:21
  37.2 6.4 %collective-permute-start.4 = (f32[4,1,1024]{2,0,1:T(4,128)S(1)}, f32[4,1,1024]{2,0,1:T(4,128)S(1)}, u32[]{:S(2)}, u32[]{:S(2)}) collective-permute-start(f32[4,1,1024]{2,0,1:T(4,128)S(1)} %get-tuple-element.174), channel_id=1, source_target_pairs={{0,2},{2,4},{4,6},{6,8},{8,10},{10,12},{12,14},{14,16},{16,18},{18... | collective-permute-start | bytes 49160 | tf_op jit(solution)/shard_map/ppermute | solution.py:20
  43.6 6.2 %collective-permute-start.6 = (f32[1,10,1024]{2,0,1:T(1,128)S(1)}, f32[1,10,1024]{2,0,1:T(1,128)S(1)}, u32[]{:S(2)}, u32[]{:S(2)}) collective-permute-start(f32[1,10,1024]{2,0,1:T(1,128)S(1)} %get-tuple-element.136), channel_id=1, source_target_pairs={{0,1},{2,3},{4,5},{6,7},{8,9},{10,11},{12,13},{14,15},{16,17},{18,... | collective-permute-start | bytes 122888 | tf_op jit(solution)/shard_map/ppermute | solution.py:20
  48.2 6.0 %collective-permute-start.7 = (f32[1,10,1024]{2,0,1:T(1,128)S(1)}, f32[1,10,1024]{2,0,1:T(1,128)S(1)}, u32[]{:S(2)}, u32[]{:S(2)}) collective-permute-start(f32[1,10,1024]{2,0,1:T(1,128)S(1)} %get-tuple-element.137), channel_id=1, source_target_pairs={{1,0},{3,2},{5,4},{7,6},{9,8},{11,10},{13,12},{15,14},{17,16},{19,... | collective-permute-start | bytes 122888 | tf_op jit(solution)/shard_map/ppermute | solution.py:21
  55.0 7.7 %collective-permute-start.9 = (f32[4,1,1024]{2,0,1:T(4,128)S(1)}, f32[4,1,1024]{2,0,1:T(4,128)S(1)}, u32[]{:S(2)}, u32[]{:S(2)}) collective-permute-start(f32[4,1,1024]{2,0,1:T(4,128)S(1)} %get-tuple-element.166), channel_id=1, source_target_pairs={{2,0},{4,2},{6,4},{8,6},{10,8},{12,10},{14,12},{16,14},{18,16},{20... | collective-permute-start | bytes 49160 | tf_op jit(solution)/shard_map/ppermute | solution.py:21
  56.3 6.4 %collective-permute-start.8 = (f32[4,1,1024]{2,0,1:T(4,128)S(1)}, f32[4,1,1024]{2,0,1:T(4,128)S(1)}, u32[]{:S(2)}, u32[]{:S(2)}) collective-permute-start(f32[4,1,1024]{2,0,1:T(4,128)S(1)} %get-tuple-element.167), channel_id=1, source_target_pairs={{0,2},{2,4},{4,6},{6,8},{8,10},{10,12},{12,14},{14,16},{16,18},{18... | collective-permute-start | bytes 49160 | tf_op jit(solution)/shard_map/ppermute | solution.py:20
  64.2 5.9 %collective-permute-start.11 = (f32[1,10,1024]{2,0,1:T(1,128)S(1)}, f32[1,10,1024]{2,0,1:T(1,128)S(1)}, u32[]{:S(2)}, u32[]{:S(2)}) collective-permute-start(f32[1,10,1024]{2,0,1:T(1,128)S(1)} %get-tuple-element.135), channel_id=1, source_target_pairs={{1,0},{3,2},{5,4},{7,6},{9,8},{11,10},{13,12},{15,14},{17,16},{19,... | collective-permute-start | bytes 122888 | tf_op jit(solution)/shard_map/ppermute | solution.py:21
  72.1 27.6 %collective-permute-start.13 = (f32[4,1,1024]{2,0,1:T(4,128)S(1)}, f32[4,1,1024]{2,0,1:T(4,128)S(1)}, u32[]{:S(2)}, u32[]{:S(2)}) collective-permute-start(f32[4,1,1024]{2,0,1:T(4,128)S(1)} %get-tuple-element.159), channel_id=1, source_target_pairs={{2,0},{4,2},{6,4},{8,6},{10,8},{12,10},{14,12},{16,14},{18,16},{20... | collective-permute-start | bytes 49160 | tf_op jit(solution)/shard_map/ppermute | solution.py:21
  73.4 26.3 %collective-permute-start.12 = (f32[4,1,1024]{2,0,1:T(4,128)S(1)}, f32[4,1,1024]{2,0,1:T(4,128)S(1)}, u32[]{:S(2)}, u32[]{:S(2)}) collective-permute-start(f32[4,1,1024]{2,0,1:T(4,128)S(1)} %get-tuple-element.160), channel_id=1, source_target_pairs={{0,2},{2,4},{4,6},{6,8},{8,10},{10,12},{12,14},{14,16},{16,18},{18... | collective-permute-start | bytes 49160 | tf_op jit(solution)/shard_map/ppermute | solution.py:20
  92.7 13.4 %all-to-all-start.1 = ((f32[16,1,2,128]{3,2,1,0:T(2,128)}), f32[16,1,2,128]{3,2,1,0:T(2,128)S(1)}, u32[]{:S(2)}, u32[]{:S(2)}) async-start(f32[16,1,2,128]{3,2,1,0:T(2,128)} %copy.690), calls=%async_computation.1 | async-start | bytes 32768 | tf_op jit(solution)/shard_map/all_to_all | solution.py:127
  99.8 7.9 %collective-permute-start.14 = (f32[1,10,1024]{2,0,1:T(1,128)S(1)}, f32[1,10,1024]{2,0,1:T(1,128)S(1)}, u32[]{:S(2)}, u32[]{:S(2)}) collective-permute-start(f32[1,10,1024]{2,0,1:T(1,128)S(1)} %get-tuple-element.132), channel_id=1, source_target_pairs={{0,1},{2,3},{4,5},{6,7},{8,9},{10,11},{12,13},{14,15},{16,17},{18,... | collective-permute-start | bytes 122888 | tf_op jit(solution)/shard_map/ppermute | solution.py:20
  102.0 5.9 %collective-permute-start.15 = (f32[1,10,1024]{2,0,1:T(1,128)S(1)}, f32[1,10,1024]{2,0,1:T(1,128)S(1)}, u32[]{:S(2)}, u32[]{:S(2)}) collective-permute-start(f32[1,10,1024]{2,0,1:T(1,128)S(1)} %get-tuple-element.133), channel_id=1, source_target_pairs={{1,0},{3,2},{5,4},{7,6},{9,8},{11,10},{13,12},{15,14},{17,16},{19,... | collective-permute-start | bytes 122888 | tf_op jit(solution)/shard_map/ppermute | solution.py:21
  108.9 7.9 %collective-permute-start.17 = (f32[4,1,1024]{2,0,1:T(4,128)S(1)}, f32[4,1,1024]{2,0,1:T(4,128)S(1)}, u32[]{:S(2)}, u32[]{:S(2)}) collective-permute-start(f32[4,1,1024]{2,0,1:T(4,128)S(1)} %get-tuple-element.152), channel_id=1, source_target_pairs={{2,0},{4,2},{6,4},{8,6},{10,8},{12,10},{14,12},{16,14},{18,16},{20... | collective-permute-start | bytes 49160 | tf_op jit(solution)/shard_map/ppermute | solution.py:21
  110.2 6.6 %collective-permute-start.16 = (f32[4,1,1024]{2,0,1:T(4,128)S(1)}, f32[4,1,1024]{2,0,1:T(4,128)S(1)}, u32[]{:S(2)}, u32[]{:S(2)}) collective-permute-start(f32[4,1,1024]{2,0,1:T(4,128)S(1)} %get-tuple-element.153), channel_id=1, source_target_pairs={{0,2},{2,4},{4,6},{6,8},{8,10},{10,12},{12,14},{14,16},{16,18},{18... | collective-permute-start | bytes 49160 | tf_op jit(solution)/shard_map/ppermute | solution.py:20
  116.8 3.7 %collective-permute-start.18 = (f32[1,10,1024]{2,0,1:T(1,128)S(1)}, f32[1,10,1024]{2,0,1:T(1,128)S(1)}, u32[]{:S(2)}, u32[]{:S(2)}) collective-permute-start(f32[1,10,1024]{2,0,1:T(1,128)S(1)} %get-tuple-element.130), channel_id=1, source_target_pairs={{0,1},{2,3},{4,5},{6,7},{8,9},{10,11},{12,13},{14,15},{16,17},{18,... | collective-permute-start | bytes 122888 | tf_op jit(solution)/shard_map/ppermute | solution.py:20
  118.8 6.3 %collective-permute-start.19 = (f32[1,10,1024]{2,0,1:T(1,128)S(1)}, f32[1,10,1024]{2,0,1:T(1,128)S(1)}, u32[]{:S(2)}, u32[]{:S(2)}) collective-permute-start(f32[1,10,1024]{2,0,1:T(1,128)S(1)} %get-tuple-element.131), channel_id=1, source_target_pairs={{1,0},{3,2},{5,4},{7,6},{9,8},{11,10},{13,12},{15,14},{17,16},{19,... | collective-permute-start | bytes 122888 | tf_op jit(solution)/shard_map/ppermute | solution.py:21
  126.0 7.9 %collective-permute-start.21 = (f32[4,1,1024]{2,0,1:T(4,128)S(1)}, f32[4,1,1024]{2,0,1:T(4,128)S(1)}, u32[]{:S(2)}, u32[]{:S(2)}) collective-permute-start(f32[4,1,1024]{2,0,1:T(4,128)S(1)} %get-tuple-element.145), channel_id=1, source_target_pairs={{2,0},{4,2},{6,4},{8,6},{10,8},{12,10},{14,12},{16,14},{18,16},{20... | collective-permute-start | bytes 49160 | tf_op jit(solution)/shard_map/ppermute | solution.py:21
  127.3 6.6 %collective-permute-start.20 = (f32[4,1,1024]{2,0,1:T(4,128)S(1)}, f32[4,1,1024]{2,0,1:T(4,128)S(1)}, u32[]{:S(2)}, u32[]{:S(2)}) collective-permute-start(f32[4,1,1024]{2,0,1:T(4,128)S(1)} %get-tuple-element.146), channel_id=1, source_target_pairs={{0,2},{2,4},{4,6},{6,8},{8,10},{10,12},{12,14},{14,16},{16,18},{18... | collective-permute-start | bytes 49160 | tf_op jit(solution)/shard_map/ppermute | solution.py:20
  135.4 6.2 %collective-permute-start.23 = (f32[1,10,1024]{2,0,1:T(1,128)S(1)}, f32[1,10,1024]{2,0,1:T(1,128)S(1)}, u32[]{:S(2)}, u32[]{:S(2)}) collective-permute-start(f32[1,10,1024]{2,0,1:T(1,128)S(1)} %get-tuple-element.129), channel_id=1, source_target_pairs={{1,0},{3,2},{5,4},{7,6},{9,8},{11,10},{13,12},{15,14},{17,16},{19,... | collective-permute-start | bytes 122888 | tf_op jit(solution)/shard_map/ppermute | solution.py:21
  (9 other events, 153.5 us)
